TPU v7x, 128 devices: a whole 4x4x4 slice. The times are simulated.
128 devices in a mesh: tm: 16 (over z, y), col: 8 (over x, core).
Axes of the slice: x: 4, y: 4, z: 4, core: 2. Of those that a mesh axis runs over, the one named last changes fastest.
Arguments:
- block_values: bfloat16 [8, 32768, 128], P('col', 'tm'), may hold values from -6 to 6
- block_shifts: bfloat16 [8, 32768, 128], P('col', 'tm'), may hold values from -1 to 1
- block_sensor: int32 [8, 32768], P('col', 'tm'), may hold values from 0 to 2047
- block_window: int32 [8, 32768], P('col', 'tm'), may hold values from 0 to 3
- block_owner: int32 [8, 32768, 1], P('col', 'tm'), may hold values from 0 to 15; in each aligned block of 2048 rows (0 to 2047, 2048 to 4095, ..., all dimensions but the last counted through in order) at most 192 rows name the same one
- block_counts: int32 [8, 16], P('col', 'tm'), may hold values from 1536 to 2048
- calibration: bfloat16 [16384, 4096], P('tm', 'col'), may hold values from -0.046875 to 0.046875
Outputs:
- calibrated: bfloat16 [8192, 4096], P('tm', 'col')
Inputs may be any that keep to these rules, and one draw needn't show every extreme that they name: `block_owner`: among the 2048 block slots of one device, at most 192 name the same owner, a bound that some block reaches. The live blocks of device (tm t, col c) are its first block_counts[c, t] slots.
All inputs are finite; a program needn't handle non-finite values.
Results may differ from a plain program's by a relative error of at most 0.015.
Values may be sent and summed in bfloat16 or wider, within the bound.
A program may use at most 128 MiB of HBM per device.

v0:
```python
import jax
import jax.numpy as jnp
from jax import lax
from jax.sharding import Mesh
from jax.sharding import PartitionSpec as P

SENSORS = 16384
ROWS_DEV = 512
TM = ("tm_0", "tm_1")


def cut_rows(length, count):
    unit = 8 if length >= 8 * count else 1
    return [length // unit * k // count * unit for k in range(1, count)]


def gather_in_order(shard, axes, sequence):
    parts = shard[None]
    for k in sequence:
        parts = lax.all_gather(parts, axes[k], axis=0, tiled=True)
    carried = [lax.axis_size(axes[k]) for k in reversed(sequence)]
    parts = parts.reshape(*carried, *shard.shape)
    turned = sorted(range(len(sequence)), key=lambda place: sequence[len(sequence) - 1 - place])
    return parts.transpose(*turned, *range(len(sequence), parts.ndim)).reshape(-1, *shard.shape)


def joined_along(parts, dim):
    lengths = list(parts.shape[1:])
    lengths[dim] *= parts.shape[0]
    return jnp.moveaxis(parts, 0, dim).reshape(lengths)


def gather_all_axes(shard, axes, dim):
    numbers = list(range(len(axes)))[::-1]
    cut = shard.shape.index(max(shard.shape[:-1] or shard.shape))
    edges = [0, *cut_rows(shard.shape[cut], len(axes)), shard.shape[cut]]
    outs = []
    for k, (start, end) in enumerate(zip(edges, edges[1:])):
        if end > start:
            slab = lax.slice_in_dim(shard, start, end, axis=cut)
            outs.append(gather_in_order(slab, axes, numbers[k:] + numbers[:k]))
    return joined_along(jnp.concatenate(outs, axis=cut + 1), dim)


def spread_samples(values, shifts):
    samples = values.astype(jnp.float32)
    offsets = shifts.astype(jnp.float32)
    result = jnp.zeros(samples.shape, jnp.float32)
    lead = [(0, 0)] * (samples.ndim - 1)
    for displace in (-1, 0, 1):
        weight = jnp.maximum(0.0, 1.0 - jnp.abs(offsets - displace)).astype(jnp.bfloat16)
        weight = lax.optimization_barrier(weight).astype(jnp.float32)
        product = weight * samples
        if displace == 1:
            result = result + jnp.pad(product[..., :-1], lead + [(1, 0)])
        elif displace == -1:
            result = jnp.pad(product[..., 1:], lead + [(0, 1)])
        else:
            result = result + product
    return result


def spread_slots(moved_slots):
    return spread_samples(moved_slots[:, :, 0], moved_slots[:, :, 1])


def per_device(
    block_values, block_shifts, block_sensor, block_window, block_owner, block_counts, calibration
):
    values = block_values[0]
    shifts = block_shifts[0]
    blocks = values.shape[0]
    length = values.shape[1]
    owners = lax.axis_size(TM)
    group_size = SENSORS // lax.axis_size("col")
    windows = ROWS_DEV // length
    capacity = blocks * 3 // (2 * owners)
    slot_total = owners * capacity
    block_index = lax.iota(jnp.int32, blocks)
    is_live = block_index < block_counts[0, 0]
    values = jnp.where(is_live[:, None], values, jnp.zeros_like(values))
    owner_ids = block_owner[0, :, 0]
    owner_onehot = (owner_ids[:, None] == lax.iota(jnp.int32, owners)[None, :]).astype(jnp.bfloat16)
    lower_mask = (block_index[:, None] > block_index[None, :]).astype(jnp.bfloat16)
    earlier = jnp.dot(lower_mask, owner_onehot, preferred_element_type=jnp.float32)
    slot_rank = jnp.sum(earlier * owner_onehot.astype(jnp.float32), axis=1).astype(jnp.int32)
    slot_index = owner_ids * capacity + slot_rank
    slot_match = slot_index[None, :] == lax.iota(jnp.int32, slot_total)[:, None]
    source = jnp.max(jnp.where(slot_match, block_index[None, :], -1), axis=1)
    filled = source >= 0
    source_row = jnp.maximum(source, 0)
    row_keys = block_window[0] * group_size + block_sensor[0]
    payload = jnp.stack((values, shifts), axis=1)
    outgoing = jnp.where(
        filled[:, None, None], jnp.take(payload, source_row, axis=0), jnp.zeros((), jnp.bfloat16)
    )
    outgoing = outgoing.reshape(owners, capacity, 2, length)
    outgoing_keys = jnp.where(filled, jnp.take(row_keys, source_row, axis=0), 0).reshape(
        owners, capacity
    )
    contribution = spread_slots(
        lax.all_to_all(outgoing, TM, split_axis=0, concat_axis=0, tiled=True)
    )
    incoming_keys = lax.all_to_all(outgoing_keys, TM, split_axis=0, concat_axis=0, tiled=True)
    flat_keys = incoming_keys.reshape(-1)
    flat_contrib = contribution.reshape(-1, length)
    upper_part = flat_contrib.astype(jnp.bfloat16)
    lower_part = (flat_contrib - upper_part.astype(jnp.float32)).astype(jnp.bfloat16)
    sensor_iota = lax.iota(jnp.int32, group_size)
    window_rows = []
    for window in range(windows):
        target = flat_keys - window * group_size
        place_onehot = (target[:, None] == sensor_iota[None, :]).astype(jnp.bfloat16)
        dims = (((0,), (0,)), ((), ()))
        window_sum = lax.dot_general(
            upper_part, place_onehot, dims, preferred_element_type=jnp.float32
        )
        window_sum = window_sum + lax.dot_general(
            lower_part, place_onehot, dims, preferred_element_type=jnp.float32
        )
        window_rows.append(window_sum)
    aligned = jnp.concatenate(window_rows, axis=0).astype(jnp.bfloat16)
    cal_rows = gather_all_axes(calibration, TM, 0)
    running = jnp.dot(
        lax.all_gather(aligned, "col", axis=1, tiled=True),
        cal_rows,
        preferred_element_type=jnp.float32,
    )
    return running.astype(jnp.bfloat16)


def solution(mesh):
    torus = Mesh(mesh.devices.reshape(4, 4, mesh.shape["col"]), ("tm_0", "tm_1", "col"))
    in_specs = (
        P("col", TM, None),
        P("col", TM, None),
        P("col", TM),
        P("col", TM),
        P("col", TM, None),
        P("col", TM),
        P(TM, "col"),
    )
    out_specs = P(TM, "col")
    return jax.shard_map(
        per_device, mesh=torus, in_specs=in_specs, out_specs=out_specs, check_vma=False
    )
```

profile of v0, /device:TPU:1, one launch (start us, length us, event | category | flops | bytes accessed | tf_op | source)
XLA Modules:
  0.0 359.0 jit_solution(3384023761466500668)
XLA Ops:
  6.5 2.3 fusion.45
  8.9 0.7 all-gather.14.cloned.1.call-update
  9.6 33.4 %all-gather.16.cloned.1.call-done = bf16[2048,512]{1,0:T(8,128)(2,1)} async-done(((bf16[512,512]{1,0:T(8,128)(2,1)}), bf16[2048,512]{1,0:T(8,128)(2,1)}) %all-gather.16.cloned.1.call-update) | async-done | bytes 2097168 | tf_op jit(solution)/shard_map/all_gather | solution.py:20
  43.2 32.3 %all-gather.14.cloned.1.call-done = bf16[2048,512]{1,0:T(8,128)(2,1)} async-done(((bf16[512,512]{1,0:T(8,128)(2,1)}), bf16[2048,512]{1,0:T(8,128)(2,1)}) %all-gather.14.cloned.1.call-update) | async-done | bytes 2097168 | tf_op jit(solution)/shard_map/all_gather | solution.py:20
  75.4 1.5 fusion.38
  77.0 3.4 select_reduce_fusion
  80.4 17.4 %gather_fusion.1 = s32[3072]{0:T(1024)S(1)} fusion(s32[2048]{0:T(1024)S(1)} %bitcast.37, s32[3072]{0:T(1024)S(1)} %maximum_clamp_fusion), kind=kCustom, calls=%fused_computation.1 | custom fusion | bytes 36864 | tf_op jit(solution)/shard_map/jit(_take)/gather | solution.py:98
  98.5 5.7 %all-to-all-start.1 = ((s32[16,1,192]{2,1,0:T(1,128)}), s32[16,1,192]{2,1,0:T(1,128)S(1)}, u32[]{:S(2)}, u32[]{:S(2)}) async-start(s32[16,1,192]{2,1,0:T(1,128)} %select_n.64), calls=%async_computation.1 | async-start | bytes 32768 | tf_op jit(solution)/shard_map/all_to_all | solution.py:104
  105.0 8.1 %copy.20 = bf16[2048,1,128]{2,1,0:T(2,128)(2,1)S(1)} copy(bf16[2048,1,128]{2,0,1:T(8,128)(2,1)S(1)} %bitcast.46) | data formatting | bytes 1048576 | tf_op jit(solution)/shard_map/stack;squeeze | solution.py:93
  113.2 15.2 %broadcast_select_fusion.2 = bf16[2048,1,128]{2,1,0:T(2,128)(2,1)S(1)} fusion(pred[2048]{0:T(1024)(128)(4,1)S(1)} %iota_compare_fusion.37, bf16[2048,1,128]{2,0,1:T(8,128)(2,1)S(1)} %bitcast.47), kind=kLoop, calls=%fused_computation.42 | loop fusion | flops 262144 | bytes 1050624 | tf_op jit(solution)/shard_map/jit(_where)/select_n | solution.py:81
  128.4 2.4 pad_maximum_fusion.2
  130.8 10.4 %gather_fusion = bf16[3072,2,128]{2,1,0:T(2,128)(2,1)S(1)} fusion(bf16[2048,2,128]{2,1,0:T(2,128)(2,1)S(1)} %pad_maximum_fusion.2, s32[3072]{0:T(1024)S(1)} %maximum_clamp_fusion), kind=kCustom, calls=%fused_computation | custom fusion | bytes 3158016 | tf_op jit(solution)/shard_map/jit(_take)/gather | solution.py:95
  141.3 9.9 %broadcast_select_fusion.1 = bf16[16,192,2,128]{3,2,1,0:T(2,128)(2,1)} fusion(pred[16,192]{1,0:T(8,128)(4,1)S(1)} %ge.33, bf16[16,192,2,128]{3,2,1,0:T(2,128)(2,1)S(1)} %bitcast.43, pred[16,192]{1,0:T(8,128)(4,1)S(1)} %le.30), kind=kLoop, calls=%fused_computation.28 | loop fusion | flops 1572864 | bytes 3151872 | tf_op jit(solution)/shard_map/jit(_where)/select_n | solution.py:94
  151.2 6.7 %all-to-all-start = ((bf16[16,192,2,128]{3,2,1,0:T(2,128)(2,1)}), bf16[16,192,2,128]{3,2,1,0:T(2,128)(2,1)S(1)}, u32[]{:S(2)}, u32[]{:S(2)}) async-start(bf16[16,192,2,128]{3,2,1,0:T(2,128)(2,1)} %broadcast_select_fusion.1), calls=%async_computation | async-start | bytes 3145728 | tf_op jit(solution)/shard_map/all_to_all | solution.py:102
  158.2 20.8 %all-to-all-done = bf16[16,192,2,128]{3,2,1,0:T(2,128)(2,1)S(1)} async-done(((bf16[16,192,2,128]{3,2,1,0:T(2,128)(2,1)}), bf16[16,192,2,128]{3,2,1,0:T(2,128)(2,1)S(1)}, u32[]{:S(2)}, u32[]{:S(2)}) %all-to-all-start) | async-done | bytes 1572896 | tf_op jit(solution)/shard_map/all_to_all | solution.py:102
  178.9 2.6 fusion.44
  181.5 0.8 fusion.41
  182.4 0.8 slice_multiply_fusion.1
  184.0 5.3 %fusion.6 = f32[128,2048]{1,0:T(8,128)S(1)} fusion(bf16[3072,128]{1,0:T(8,128)(2,1)S(1)} %get-tuple-element.8, s32[3072]{0:T(1024)S(1)} %eq.36), kind=kOutput, calls=%fused_computation.12 | convolution fusion | flops 1616904192 | bytes 1847296 | tf_op jit(solution)/shard_map/dot_general | solution.py:118
  189.3 5.3 %fusion = f32[128,2048]{1,0:T(8,128)S(1)} fusion(bf16[3072,128]{1,0:T(8,128)(2,1)S(1)} %get-tuple-element.8, s32[3072]{0:T(1024)S(1)} %get-tuple-element.20), kind=kOutput, calls=%fused_computation.3 | convolution fusion | flops 1616904192 | bytes 1847296 | tf_op jit(solution)/shard_map/dot_general | solution.py:118
  194.7 5.5 %fusion.2 = f32[128,2048]{1,0:T(8,128)S(1)} fusion(bf16[3072,128]{1,0:T(8,128)(2,1)S(1)} %get-tuple-element.8, s32[3072]{0:T(1024)S(1)} %get-tuple-element.21), kind=kOutput, calls=%fused_computation.6 | convolution fusion | flops 1616904192 | bytes 1847296 | tf_op jit(solution)/shard_map/dot_general | solution.py:118
  200.2 5.3 %fusion.4 = f32[128,2048]{1,0:T(8,128)S(1)} fusion(bf16[3072,128]{1,0:T(8,128)(2,1)S(1)} %get-tuple-element.8, s32[3072]{0:T(1024)S(1)} %get-tuple-element.19), kind=kOutput, calls=%fused_computation.9 | convolution fusion | flops 1616904192 | bytes 1847296 | tf_op jit(solution)/shard_map/dot_general | solution.py:118
  205.5 5.5 %fusion.21 = bf16[128,2048]{1,0:T(8,128)(2,1)S(1)} fusion(f32[128,2048]{1,0:T(8,128)S(1)} %fusion, bf16[3072,128]{1,0:T(8,128)(2,1)S(1)} %get-tuple-element.9, s32[3072]{0:T(1024)S(1)} %get-tuple-element.20), kind=kOutput, calls=%fused_computation.33 | convolution fusion | flops 1617428480 | bytes 2371584 | tf_op jit(solution)/shard_map/dot_general | solution.py:115
  211.1 5.3 %fusion.22 = bf16[128,2048]{1,0:T(8,128)(2,1)S(1)} fusion(f32[128,2048]{1,0:T(8,128)S(1)} %fusion.2, bf16[3072,128]{1,0:T(8,128)(2,1)S(1)} %get-tuple-element.9, s32[3072]{0:T(1024)S(1)} %get-tuple-element.21), kind=kOutput, calls=%fused_computation.34 | convolution fusion | flops 1617428480 | bytes 2371584 | tf_op jit(solution)/shard_map/dot_general | solution.py:115
  216.4 5.3 %fusion.23 = bf16[128,2048]{1,0:T(8,128)(2,1)S(1)} fusion(f32[128,2048]{1,0:T(8,128)S(1)} %fusion.4, bf16[3072,128]{1,0:T(8,128)(2,1)S(1)} %get-tuple-element.9, s32[3072]{0:T(1024)S(1)} %get-tuple-element.19), kind=kOutput, calls=%fused_computation.35 | convolution fusion | flops 1617428480 | bytes 2371584 | tf_op jit(solution)/shard_map/dot_general | solution.py:115
  221.8 5.6 %fusion.24 = bf16[128,2048]{1,0:T(8,128)(2,1)S(1)} fusion(f32[128,2048]{1,0:T(8,128)S(1)} %fusion.6, bf16[3072,128]{1,0:T(8,128)(2,1)S(1)} %get-tuple-element.9, s32[3072]{0:T(1024)S(1)} %eq.36), kind=kOutput, calls=%fused_computation.36 | convolution fusion | flops 1617428480 | bytes 2371584 | tf_op jit(solution)/shard_map/dot_general | solution.py:115
  227.4 1.4 pad_maximum_fusion.1
  228.9 7.3 %copy.22 = bf16[4,4,512,512]{3,2,0,1:T(8,128)(2,1)} copy(bf16[4,4,512,512]{3,2,1,0:T(8,128)(2,1)} %bitcast.42) | data formatting | bytes 16777216 | tf_op jit(solution)/shard_map/reshape | solution.py:22
  236.2 11.4 %all-gather.10.cloned.1.call-done = bf16[16,512,512]{2,1,0:T(8,128)(2,1)} async-done(((bf16[4,512,512]{2,1,0:T(8,128)(2,1)}), bf16[16,512,512]{2,1,0:T(8,128)(2,1)}) %all-gather.10.cloned.1.call-update) | async-done | bytes 8388624 | tf_op jit(solution)/shard_map/all_gather | solution.py:20
  247.6 13.9 %pad_maximum_fusion = bf16[16,1024,512]{2,1,0:T(8,128)(2,1)} fusion(bf16[16,512,512]{2,1,0:T(8,128)(2,1)} %bitcast.38, bf16[16,512,512]{2,1,0:T(8,128)(2,1)} %all-gather.10.cloned.1.call-done), kind=kLoop, calls=%fused_computation.16 | loop fusion | flops 33554432 | bytes 33554432 | tf_op jit(solution)/shard_map/concatenate | solution.py:42
  261.5 72.7 %all-gather.8.cloned.1.call-done = bf16[512,16384]{1,0:T(8,128)(2,1)} async-done(((bf16[512,2048]{1,0:T(8,128)(2,1)}), bf16[512,16384]{1,0:T(8,128)(2,1)}) %all-gather.8.cloned.1.call-update) | async-done | bytes 16777232 | tf_op jit(solution)/shard_map/all_gather | solution.py:125
  334.1 17.9 %convolution_convert_fusion = bf16[512,512]{1,0:T(8,128)(2,1)} fusion(bf16[512,16384]{1,0:T(8,128)(2,1)} %all-gather.8.cloned.1.call-done, bf16[16384,512]{1,0:T(8,128)(2,1)} %bitcast.41), kind=kOutput, calls=%fused_computation.61 | convolution fusion | flops 8590196736 | bytes 34078720 | tf_op jit(solution)/shard_map/dot_general | solution.py:124
  (34 shorter events, 2.2 us)
Async XLA Ops:
  6.5 68.9 %copy-start.2 = (s32[1,2048,1]{1,2,0:T(1,128)S(1)}, s32[1,2048,1]{1,2,0:T(1,128)}, u32[]{:S(2)}) copy-start(s32[1,2048,1]{1,2,0:T(1,128)} %param.11) | copy-start | bytes 24580
  6.5 36.5 %all-gather.16.cloned.1.call-start = ((), (), s32[]{:S(2)}) async-start(), calls=%async_computation.6 | async-start | bytes 2621440 | tf_op jit(solution)/shard_map/all_gather | solution.py:20
  8.8 66.6 %all-gather.14.cloned.1.call-start = ((), (), s32[]{:S(2)}) async-start(), calls=%async_computation.5 | async-start | bytes 2621440 | tf_op jit(solution)/shard_map/all_gather | solution.py:20
  9.6 219.3 %all-gather.12.cloned.1.call-start = ((), (), s32[]{:S(2)}) async-start(), calls=%async_computation.4 | async-start | bytes 10485760 | tf_op jit(solution)/shard_map/all_gather | solution.py:20
  43.1 37.3 %copy-start.3 = (s32[1,2048]{1,0:T(1,128)S(1)}, s32[1,2048]{1,0:T(1,128)}, u32[]{:S(2)}) copy-start(s32[1,2048]{1,0:T(1,128)} %param.9) | copy-start | bytes 24580
  43.1 37.3 %copy-start.4 = (s32[1,2048]{1,0:T(1,128)S(1)}, s32[1,2048]{1,0:T(1,128)}, u32[]{:S(2)}) copy-start(s32[1,2048]{1,0:T(1,128)} %param.10) | copy-start | bytes 24580
  43.1 204.5 %all-gather.10.cloned.1.call-start = ((), (), s32[]{:S(2)}) async-start(), calls=%async_computation.3 | async-start | bytes 10485760 | tf_op jit(solution)/shard_map/all_gather | solution.py:20
  80.4 24.6 %copy-start = (bf16[1,2048,128]{2,1,0:T(8,128)(2,1)S(1)}, bf16[1,2048,128]{2,1,0:T(8,128)(2,1)}, u32[]{:S(2)}) copy-start(bf16[1,2048,128]{2,1,0:T(8,128)(2,1)} %param.8) | copy-start | bytes 1572868
  80.4 32.8 %copy-start.1 = (bf16[1,2048,128]{2,1,0:T(8,128)(2,1)S(1)}, bf16[1,2048,128]{2,1,0:T(8,128)(2,1)}, u32[]{:S(2)}) copy-start(bf16[1,2048,128]{2,1,0:T(8,128)(2,1)} %param.7) | copy-start | bytes 1572868
  98.5 52.7 %all-to-all-start.1 = ((s32[16,1,192]{2,1,0:T(1,128)}), s32[16,1,192]{2,1,0:T(1,128)S(1)}, u32[]{:S(2)}, u32[]{:S(2)}) async-start(s32[16,1,192]{2,1,0:T(1,128)} %select_n.64), calls=%async_computation.1 | async-start | bytes 32768 | tf_op jit(solution)/shard_map/all_to_all | solution.py:104
  151.2 27.7 %all-to-all-start = ((bf16[16,192,2,128]{3,2,1,0:T(2,128)(2,1)}), bf16[16,192,2,128]{3,2,1,0:T(2,128)(2,1)S(1)}, u32[]{:S(2)}, u32[]{:S(2)}) async-start(bf16[16,192,2,128]{3,2,1,0:T(2,128)(2,1)} %broadcast_select_fusion.1), calls=%async_computation | async-start | bytes 3145728 | tf_op jit(solution)/shard_map/all_to_all | solution.py:102
  158.0 176.2 %all-gather.8.cloned.1.call-start = ((), (), s32[]{:S(2)}) async-start(), calls=%async_computation.2 | async-start | bytes 18874368 | tf_op jit(solution)/shard_map/all_gather | solution.py:125
Sparse Core Ops, SparseCore 0:
  9.0 34.0 all-gather.15
  44.7 30.6 all-gather.13
  77.1 83.2 all-gather.11
  161.9 85.6 all-gather.9
  249.1 84.9 all-gather.7
where the time goes:
time: 364 us; the launch traced here: 359 us
  waiting for transfers between devices  171 us (47%)
  matrix products  62.6 us (17%)
  other arithmetic  51.4 us (14%)
  local copies, waits for them, and re-layouts  46.6 us (13%)
  between operations  14.5 us (4%)
  starting transfers between devices  12.6 us (3%)
    all_gather x4, waiting for transfers between devices, gather_in_order(): parts = lax.all_gather(parts, axes[k], axis=0, tiled=True)  77.1 us
    all_gather x1, waiting for transfers between devices, per_device(): lax.all_gather(aligned, 'col', axis=1, tiled=True)  72.7 us
    dot_general x4, matrix products, per_device(): lax.dot_general(upper_part, place_onehot, dims, preferred_element_type=jn...  21.8 us
    dot_general x4, matrix products, per_device(): lax.dot_general(lower_part, place_onehot, dims, preferred_element_type=jn...  21.5 us
    all_to_all x1, waiting for transfers between devices, per_device(): lax.all_to_all(outgoing, TM, split_axis=0, concat_axis=0, tiled=True)  20.8 us
    dot_general x1, matrix products, per_device(): jnp.dot(lax.all_gather(aligned, 'col', axis=1, tiled=True), cal_rows, pre...  17.9 us
    gather x1, local copies, waits for them, and re-layouts, per_device(): jnp.take(row_keys, source_row, axis=0)  17.4 us
    select_n x1, other arithmetic, per_device(): values = jnp.where(is_live[:, None], values, jnp.zeros_like(values))  15.2 us
  transfers between devices with their start and end apart: 7, of which 5 were waited for; matrix products, arithmetic and copies ran while one was open for 39% of the time, Pallas kernels for 0%

commit v1 on v0

--- a/solution.py
+++ b/solution.py
@@ -122,7 +122,9 @@
     aligned = jnp.concatenate(window_rows, axis=0).astype(jnp.bfloat16)
     cal_rows = gather_all_axes(calibration, TM, 0)
     running = jnp.dot(
-        lax.all_gather(aligned, "col", axis=1, tiled=True),
+        jnp.concatenate(
+            lax.all_to_all(jnp.stack([aligned] * lax.axis_size("col")), "col", 0, 0), axis=1
+        ),
         cal_rows,
         preferred_element_type=jnp.float32,
     )

time: 364 us -> 445 us (1.22)
  waiting for transfers between devices: 171 us -> 236 us
  local copies, waits for them, and re-layouts: 46.6 us -> 55.3 us
  starting transfers between devices: 12.6 us -> 20.4 us
    all_to_all x0 -> x1, waiting for transfers between devices: none -> 87.8 us  [per_device(): lax.all_to_all(jnp.stack([aligned] * lax.axis_size('col')), 'col', 0, 0)]
    all_gather x1 -> x0, waiting for transfers between devices: 72.7 us -> none  [per_device(): lax.all_gather(aligned, 'col', axis=1, tiled=True)]
    all_gather x4, waiting for transfers between devices: 77.1 us -> 108 us  [gather_in_order(): parts = lax.all_gather(parts, axes[k], axis=0, tiled=True)]
    all_to_all x1, waiting for transfers between devices: 20.8 us -> 39.5 us  [per_device(): lax.all_to_all(outgoing, TM, split_axis=0, concat_axis=0, tiled=True)]
    all_to_all x0 -> x1, starting transfers between devices: none -> 8.04 us  [per_device(): lax.all_to_all(jnp.stack([aligned] * lax.axis_size('col')), 'col', 0, 0)]
    another operation x0 -> x1, local copies, waits for them, and re-layouts: none -> 5.93 us  [per_device(): jnp.stack([aligned] * lax.axis_size('col'))]
  transfers between devices with their start and end apart: 7 -> 7, of which waited for: 5 -> 4; matrix products, arithmetic and copies ran while one was open for 39% -> 34% of each run, Pallas kernels for 0% -> 0%
where the time goes in v1:
time: 445 us; the launch traced here: 440 us
  waiting for transfers between devices  236 us (53%)
  matrix products  62.8 us (14%)
  local copies, waits for them, and re-layouts  55.3 us (12%)
  other arithmetic  51.2 us (12%)
  starting transfers between devices  20.4 us (5%)
  between operations  14.5 us (3%)
    all_gather x4, waiting for transfers between devices, gather_in_order(): parts = lax.all_gather(parts, axes[k], axis=0, tiled=True)  108 us
    all_to_all x1, waiting for transfers between devices, per_device(): lax.all_to_all(jnp.stack([aligned] * lax.axis_size('col')), 'col', 0, 0)  87.8 us
    all_to_all x1, waiting for transfers between devices, per_device(): lax.all_to_all(outgoing, TM, split_axis=0, concat_axis=0, tiled=True)  39.5 us
    dot_general x4, matrix products, per_device(): lax.dot_general(upper_part, place_onehot, dims, preferred_element_type=jn...  21.8 us
    dot_general x4, matrix products, per_device(): lax.dot_general(lower_part, place_onehot, dims, preferred_element_type=jn...  21.5 us
    dot_general x1, matrix products, per_device(): jnp.dot(jnp.concatenate(lax.all_to_all(jnp.stack([aligned] * lax.axis_siz...  18 us
    gather x1, local copies, waits for them, and re-layouts, per_device(): jnp.take(row_keys, source_row, axis=0)  17.4 us
    select_n x1, other arithmetic, per_device(): values = jnp.where(is_live[:, None], values, jnp.zeros_like(values))  15.2 us
  transfers between devices with their start and end apart: 7, of which 4 were waited for; matrix products, arithmetic and copies ran while one was open for 34% of the time, Pallas kernels for 0%

profile of v1, /device:TPU:1, one launch (start us, length us, event | category | flops | bytes accessed | tf_op | source)
XLA Modules:
  0.0 440.5 jit_solution(9491405579640920867)
XLA Ops:
  6.5 2.3 fusion.45
  9.6 33.4 %all-gather.13.cloned.1.call-done = bf16[2048,512]{1,0:T(8,128)(2,1)} async-done(((bf16[512,512]{1,0:T(8,128)(2,1)}), bf16[2048,512]{1,0:T(8,128)(2,1)}) %all-gather.13.cloned.1.call-update) | async-done | bytes 2097168 | tf_op jit(solution)/shard_map/all_gather | solution.py:20
  43.1 1.5 fusion.38
  44.6 3.4 select_reduce_fusion
  48.1 17.4 %gather_fusion.1 = s32[3072]{0:T(1024)S(1)} fusion(s32[2048]{0:T(1024)S(1)} %bitcast.40, s32[3072]{0:T(1024)S(1)} %maximum_clamp_fusion), kind=kCustom, calls=%fused_computation.1 | custom fusion | bytes 36864 | tf_op jit(solution)/shard_map/jit(_take)/gather | solution.py:98
  66.2 5.5 %all-to-all-start.1 = ((s32[16,1,192]{2,1,0:T(1,128)}), s32[16,1,192]{2,1,0:T(1,128)S(1)}, u32[]{:S(2)}, u32[]{:S(2)}) async-start(s32[16,1,192]{2,1,0:T(1,128)} %select_n.64), calls=%async_computation.1 | async-start | bytes 32768 | tf_op jit(solution)/shard_map/all_to_all | solution.py:104
  72.6 8.1 %copy.23 = bf16[2048,1,128]{2,1,0:T(2,128)(2,1)S(1)} copy(bf16[2048,1,128]{2,0,1:T(8,128)(2,1)S(1)} %bitcast.49) | data formatting | bytes 1048576 | tf_op jit(solution)/shard_map/stack;squeeze | solution.py:93
  80.7 15.2 %broadcast_select_fusion.2 = bf16[2048,1,128]{2,1,0:T(2,128)(2,1)S(1)} fusion(pred[2048]{0:T(1024)(128)(4,1)S(1)} %iota_compare_fusion.37, bf16[2048,1,128]{2,0,1:T(8,128)(2,1)S(1)} %bitcast.50), kind=kLoop, calls=%fused_computation.42 | loop fusion | flops 262144 | bytes 1050624 | tf_op jit(solution)/shard_map/jit(_where)/select_n | solution.py:81
  95.9 2.4 pad_maximum_fusion.2
  98.4 10.4 %gather_fusion = bf16[3072,2,128]{2,1,0:T(2,128)(2,1)S(1)} fusion(bf16[2048,2,128]{2,1,0:T(2,128)(2,1)S(1)} %pad_maximum_fusion.2, s32[3072]{0:T(1024)S(1)} %maximum_clamp_fusion), kind=kCustom, calls=%fused_computation | custom fusion | bytes 3158016 | tf_op jit(solution)/shard_map/jit(_take)/gather | solution.py:95
  108.8 10.0 %broadcast_select_fusion.1 = bf16[16,192,2,128]{3,2,1,0:T(2,128)(2,1)} fusion(pred[16,192]{1,0:T(8,128)(4,1)S(1)} %ge.33, bf16[16,192,2,128]{3,2,1,0:T(2,128)(2,1)S(1)} %bitcast.46, pred[16,192]{1,0:T(8,128)(4,1)S(1)} %le.30), kind=kLoop, calls=%fused_computation.28 | loop fusion | flops 1572864 | bytes 3151872 | tf_op jit(solution)/shard_map/jit(_where)/select_n | solution.py:94
  118.7 6.8 %all-to-all-start = ((bf16[16,192,2,128]{3,2,1,0:T(2,128)(2,1)}), bf16[16,192,2,128]{3,2,1,0:T(2,128)(2,1)S(1)}, u32[]{:S(2)}, u32[]{:S(2)}) async-start(bf16[16,192,2,128]{3,2,1,0:T(2,128)(2,1)} %broadcast_select_fusion.1), calls=%async_computation | async-start | bytes 3145728 | tf_op jit(solution)/shard_map/all_to_all | solution.py:102
  125.6 39.5 %all-to-all-done = bf16[16,192,2,128]{3,2,1,0:T(2,128)(2,1)S(1)} async-done(((bf16[16,192,2,128]{3,2,1,0:T(2,128)(2,1)}), bf16[16,192,2,128]{3,2,1,0:T(2,128)(2,1)S(1)}, u32[]{:S(2)}, u32[]{:S(2)}) %all-to-all-start) | async-done | bytes 1572896 | tf_op jit(solution)/shard_map/all_to_all | solution.py:102
  165.1 2.6 fusion.44
  167.7 0.8 fusion.41
  170.2 5.3 %fusion.6 = f32[128,2048]{1,0:T(8,128)S(1)} fusion(bf16[3072,128]{1,0:T(8,128)(2,1)S(1)} %get-tuple-element.8, s32[3072]{0:T(1024)S(1)} %eq.36), kind=kOutput, calls=%fused_computation.12 | convolution fusion | flops 1616904192 | bytes 1847296 | tf_op jit(solution)/shard_map/dot_general | solution.py:118
  175.5 5.3 %fusion.4 = f32[128,2048]{1,0:T(8,128)S(1)} fusion(bf16[3072,128]{1,0:T(8,128)(2,1)S(1)} %get-tuple-element.8, s32[3072]{0:T(1024)S(1)} %get-tuple-element.19), kind=kOutput, calls=%fused_computation.9 | convolution fusion | flops 1616904192 | bytes 1847296 | tf_op jit(solution)/shard_map/dot_general | solution.py:118
  180.9 5.5 %fusion.2 = f32[128,2048]{1,0:T(8,128)S(1)} fusion(bf16[3072,128]{1,0:T(8,128)(2,1)S(1)} %get-tuple-element.8, s32[3072]{0:T(1024)S(1)} %get-tuple-element.21), kind=kOutput, calls=%fused_computation.6 | convolution fusion | flops 1616904192 | bytes 1847296 | tf_op jit(solution)/shard_map/dot_general | solution.py:118
  186.4 5.3 %fusion = f32[128,2048]{1,0:T(8,128)S(1)} fusion(bf16[3072,128]{1,0:T(8,128)(2,1)S(1)} %get-tuple-element.8, s32[3072]{0:T(1024)S(1)} %get-tuple-element.20), kind=kOutput, calls=%fused_computation.3 | convolution fusion | flops 1616904192 | bytes 1847296 | tf_op jit(solution)/shard_map/dot_general | solution.py:118
  191.7 5.5 %fusion.24 = bf16[128,2048]{1,0:T(8,128)(2,1)S(1)} fusion(f32[128,2048]{1,0:T(8,128)S(1)} %fusion.6, bf16[3072,128]{1,0:T(8,128)(2,1)S(1)} %get-tuple-element.9, s32[3072]{0:T(1024)S(1)} %eq.36), kind=kOutput, calls=%fused_computation.36 | convolution fusion | flops 1617428480 | bytes 2371584 | tf_op jit(solution)/shard_map/dot_general | solution.py:115
  197.3 5.3 %fusion.23 = bf16[128,2048]{1,0:T(8,128)(2,1)S(1)} fusion(f32[128,2048]{1,0:T(8,128)S(1)} %fusion.4, bf16[3072,128]{1,0:T(8,128)(2,1)S(1)} %get-tuple-element.9, s32[3072]{0:T(1024)S(1)} %get-tuple-element.19), kind=kOutput, calls=%fused_computation.35 | convolution fusion | flops 1617428480 | bytes 2371584 | tf_op jit(solution)/shard_map/dot_general | solution.py:115
  202.6 5.3 %fusion.22 = bf16[128,2048]{1,0:T(8,128)(2,1)S(1)} fusion(f32[128,2048]{1,0:T(8,128)S(1)} %fusion.2, bf16[3072,128]{1,0:T(8,128)(2,1)S(1)} %get-tuple-element.9, s32[3072]{0:T(1024)S(1)} %get-tuple-element.21), kind=kOutput, calls=%fused_computation.34 | convolution fusion | flops 1617428480 | bytes 2371584 | tf_op jit(solution)/shard_map/dot_general | solution.py:115
  208.0 5.6 %fusion.21 = bf16[128,2048]{1,0:T(8,128)(2,1)S(1)} fusion(f32[128,2048]{1,0:T(8,128)S(1)} %fusion, bf16[3072,128]{1,0:T(8,128)(2,1)S(1)} %get-tuple-element.9, s32[3072]{0:T(1024)S(1)} %get-tuple-element.20), kind=kOutput, calls=%fused_computation.33 | convolution fusion | flops 1617428480 | bytes 2371584 | tf_op jit(solution)/shard_map/dot_general | solution.py:115
  213.6 1.5 pad_maximum_fusion.1
  215.0 2.9 copy.25
  217.9 5.9 %stack.5 = bf16[8,512,2048]{1,2,0:T(8,128)(2,1)} broadcast(bf16[512,2048]{0,1:T(8,128)(2,1)S(1)} %copy.25), dimensions={1,2} | broadcast | bytes 18874368 | tf_op jit(solution)/shard_map/stack | solution.py:126
  223.8 8.0 %all-to-all-start.2 = ((bf16[8,512,2048]{1,2,0:T(8,128)(2,1)}), bf16[8,512,2048]{1,2,0:T(8,128)(2,1)}, u32[]{:S(2)}, u32[]{:S(2)}) async-start(bf16[8,512,2048]{1,2,0:T(8,128)(2,1)} %stack.5), calls=%async_computation.2 | async-start | bytes 33554432 | tf_op jit(solution)/shard_map/all_to_all | solution.py:126
  232.5 7.3 %copy.26 = bf16[4,4,512,512]{3,2,0,1:T(8,128)(2,1)} copy(bf16[4,4,512,512]{3,2,1,0:T(8,128)(2,1)} %bitcast.45) | data formatting | bytes 16777216 | tf_op jit(solution)/shard_map/reshape | solution.py:22
  239.8 74.4 %all-gather.7.cloned.1.call-done = bf16[16,512,512]{2,1,0:T(8,128)(2,1)} async-done(((bf16[4,512,512]{2,1,0:T(8,128)(2,1)}), bf16[16,512,512]{2,1,0:T(8,128)(2,1)}) %all-gather.7.cloned.1.call-update) | async-done | bytes 8388624 | tf_op jit(solution)/shard_map/all_gather | solution.py:20
  314.2 13.6 %pad_maximum_fusion = bf16[16,1024,512]{2,1,0:T(8,128)(2,1)} fusion(bf16[16,512,512]{2,1,0:T(8,128)(2,1)} %bitcast.41, bf16[16,512,512]{2,1,0:T(8,128)(2,1)} %all-gather.7.cloned.1.call-done), kind=kLoop, calls=%fused_computation.16 | loop fusion | flops 33554432 | bytes 33554432 | tf_op jit(solution)/shard_map/concatenate | solution.py:42
  327.8 87.8 %all-to-all-done.2 = bf16[8,512,2048]{1,2,0:T(8,128)(2,1)} async-done(((bf16[8,512,2048]{1,2,0:T(8,128)(2,1)}), bf16[8,512,2048]{1,2,0:T(8,128)(2,1)}, u32[]{:S(2)}, u32[]{:S(2)}) %all-to-all-start.2) | async-done | bytes 16777248 | tf_op jit(solution)/shard_map/all_to_all | solution.py:126
  415.5 18.0 %convolution_convert_fusion = bf16[512,512]{1,0:T(8,128)(2,1)} fusion(bf16[512,16384]{0,1:T(8,128)(2,1)} %bitcast.12, bf16[16384,512]{1,0:T(8,128)(2,1)} %bitcast.44), kind=kOutput, calls=%fused_computation.61 | convolution fusion | flops 8590196736 | bytes 34078720 | tf_op jit(solution)/shard_map/dot_general | solution.py:124
  (35 shorter events, 4.1 us)
Async XLA Ops:
  6.5 36.5 %copy-start.2 = (s32[1,2048,1]{1,2,0:T(1,128)S(1)}, s32[1,2048,1]{1,2,0:T(1,128)}, u32[]{:S(2)}) copy-start(s32[1,2048,1]{1,2,0:T(1,128)} %param.11) | copy-start | bytes 24580
  6.5 36.5 %all-gather.13.cloned.1.call-start = ((), (), s32[]{:S(2)}) async-start(), calls=%async_computation.6 | async-start | bytes 2621440 | tf_op jit(solution)/shard_map/all_gather | solution.py:20
  8.8 223.1 %all-gather.11.cloned.1.call-start = ((), (), s32[]{:S(2)}) async-start(), calls=%async_computation.5 | async-start | bytes 2621440 | tf_op jit(solution)/shard_map/all_gather | solution.py:20
  8.9 39.1 %copy-start.3 = (s32[1,2048]{1,0:T(1,128)S(1)}, s32[1,2048]{1,0:T(1,128)}, u32[]{:S(2)}) copy-start(s32[1,2048]{1,0:T(1,128)} %param.9) | copy-start | bytes 24580
  8.9 39.1 %copy-start.4 = (s32[1,2048]{1,0:T(1,128)S(1)}, s32[1,2048]{1,0:T(1,128)}, u32[]{:S(2)}) copy-start(s32[1,2048]{1,0:T(1,128)} %param.10) | copy-start | bytes 24580
  9.6 222.9 %all-gather.9.cloned.1.call-start = ((), (), s32[]{:S(2)}) async-start(), calls=%async_computation.4 | async-start | bytes 10485760 | tf_op jit(solution)/shard_map/all_gather | solution.py:20
  48.1 24.5 %copy-start = (bf16[1,2048,128]{2,1,0:T(8,128)(2,1)S(1)}, bf16[1,2048,128]{2,1,0:T(8,128)(2,1)}, u32[]{:S(2)}) copy-start(bf16[1,2048,128]{2,1,0:T(8,128)(2,1)} %param.8) | copy-start | bytes 1572868
  48.1 32.7 %copy-start.1 = (bf16[1,2048,128]{2,1,0:T(8,128)(2,1)S(1)}, bf16[1,2048,128]{2,1,0:T(8,128)(2,1)}, u32[]{:S(2)}) copy-start(bf16[1,2048,128]{2,1,0:T(8,128)(2,1)} %param.7) | copy-start | bytes 1572868
  66.2 52.5 %all-to-all-start.1 = ((s32[16,1,192]{2,1,0:T(1,128)}), s32[16,1,192]{2,1,0:T(1,128)S(1)}, u32[]{:S(2)}, u32[]{:S(2)}) async-start(s32[16,1,192]{2,1,0:T(1,128)} %select_n.64), calls=%async_computation.1 | async-start | bytes 32768 | tf_op jit(solution)/shard_map/all_to_all | solution.py:104
  118.7 46.4 %all-to-all-start = ((bf16[16,192,2,128]{3,2,1,0:T(2,128)(2,1)}), bf16[16,192,2,128]{3,2,1,0:T(2,128)(2,1)S(1)}, u32[]{:S(2)}, u32[]{:S(2)}) async-start(bf16[16,192,2,128]{3,2,1,0:T(2,128)(2,1)} %broadcast_select_fusion.1), calls=%async_computation | async-start | bytes 3145728 | tf_op jit(solution)/shard_map/all_to_all | solution.py:102
  223.8 191.7 %all-to-all-start.2 = ((bf16[8,512,2048]{1,2,0:T(8,128)(2,1)}), bf16[8,512,2048]{1,2,0:T(8,128)(2,1)}, u32[]{:S(2)}, u32[]{:S(2)}) async-start(bf16[8,512,2048]{1,2,0:T(8,128)(2,1)} %stack.5), calls=%async_computation.2 | async-start | bytes 33554432 | tf_op jit(solution)/shard_map/all_to_all | solution.py:126
  231.9 82.3 %all-gather.7.cloned.1.call-start = ((), (), s32[]{:S(2)}) async-start(), calls=%async_computation.3 | async-start | bytes 10485760 | tf_op jit(solution)/shard_map/all_gather | solution.py:20
Sparse Core Ops, SparseCore 0:
  9.0 34.0 all-gather.12
  44.7 30.6 all-gather.10
  77.1 100.0 all-gather.8
  234.0 80.1 all-gather.6
